TPU v7x, 32 devices: a whole 2x2x4 slice. The times are simulated.
32 devices in a mesh: row: 16 (over z, x, core), col: 2 (over y).
Axes of the slice: x: 2, y: 2, z: 4, core: 2. Of those that a mesh axis runs over, the one named last changes fastest.
Arguments:
- occupied_waves: bfloat16 [1024, 32768], P('row', 'col'), may hold values from -6 to 6
- virtual_waves: bfloat16 [512, 32768], P('row', 'col'), may hold values from -6 to 6
- occupied_decay: float32 [1024], replicated, may hold values from 0.02 to 1
- virtual_decay: float32 [512], replicated, may hold values from 0.02 to 1
Outputs:
- spectrum_real: float32 [512, 32, 1024], P('row', 'col')
- spectrum_imaginary: float32 [512, 32, 1024], P('row', 'col')
All inputs are finite; a program needn't handle non-finite values.
Results may differ from a plain program's by a relative error of at most 0.0041.
Values may be sent and summed in bfloat16 or wider, within the bound.
A program may use at most 128 MiB of HBM per device.

v0:
```python
import math

import jax
import jax.numpy as jnp
from jax import lax
from jax.sharding import PartitionSpec as P

NOCC = 1024
NVIR = 512
NA = 32
NB = 32
NC = 32
ROWS_DEV = 32
NGRID = 32768


def tables(length):
    index = jnp.arange(length, dtype=jnp.int32)
    phase = index[:, None] * index[None, :] % length
    angle = phase.astype(jnp.float32) * (2.0 * math.pi / length)
    return (jnp.cos(angle), jnp.sin(angle))


def apply_table(form, data, table):
    return jnp.einsum(form, data, table, precision=lax.Precision.HIGHEST)


def real_step(data, form, length):
    cosine, sine = tables(length)
    return (apply_table(form, data, cosine), -apply_table(form, data, sine))


def complex_step(real_part, imag_part, form, length):
    cosine, sine = tables(length)
    new_real = apply_table(form, real_part, cosine) + apply_table(form, imag_part, sine)
    new_imag = apply_table(form, imag_part, cosine) - apply_table(form, real_part, sine)
    return (new_real, new_imag)


def scale_rows(waves, decay):
    return (waves * decay[:, None]).astype(jnp.bfloat16)


def place(waves, window, start_col):
    block_cols = waves.shape[1]
    buffer = jnp.zeros((waves.shape[0], window + block_cols), jnp.bfloat16)
    buffer = lax.dynamic_update_slice(buffer, waves, (jnp.int32(0), start_col))
    return buffer[:, :window]


def on_device(occupied_waves, virtual_waves, occupied_decay, virtual_decay):
    block_cols = occupied_waves.shape[1]
    row_count = lax.axis_size("row")
    contract = (((0,), (0,)), ((), ()))
    factor = -1.0 / math.sqrt(NOCC * NVIR)
    window = ROWS_DEV * row_count
    start_col = lax.axis_index("col") * block_cols
    plane_cols = NB * NC
    per_col = block_cols // plane_cols
    spread = row_count // per_col
    sub_rows = ROWS_DEV // spread

    def spread_planes(waves):
        share = waves.shape[0]
        shaped = waves.reshape(share, per_col, 1, plane_cols)
        shaped = jnp.broadcast_to(shaped, (share, per_col, spread, plane_cols))
        return shaped.reshape(share, row_count * plane_cols)

    def pick_rows(waves):
        share = waves.shape[0]
        shaped = place(waves, window, start_col).reshape(share, row_count, spread, sub_rows)
        shaped = jnp.transpose(shaped, (0, 2, 1, 3))[:, None]
        shaped = jnp.broadcast_to(shaped, (share, per_col, spread, row_count, sub_rows))
        return shaped.reshape(share, row_count * row_count * sub_rows)

    plane_occ, plane_vir = (
        lax.all_to_all(
            spread_planes(occupied_waves), "row", split_axis=1, concat_axis=0, tiled=True
        ),
        lax.all_to_all(
            spread_planes(virtual_waves), "row", split_axis=1, concat_axis=0, tiled=True
        ),
    )
    part_occ, part_vir = (
        lax.all_to_all(pick_rows(occupied_waves), "row", split_axis=1, concat_axis=0, tiled=True),
        lax.all_to_all(pick_rows(virtual_waves), "row", split_axis=1, concat_axis=0, tiled=True),
    )
    occ_rows, vir_rows = (
        lax.psum(part_occ.astype(jnp.float32).astype(jnp.bfloat16), "col").astype(jnp.float32),
        lax.psum(part_vir.astype(jnp.float32).astype(jnp.bfloat16), "col").astype(jnp.float32),
    )
    occ_rows = scale_rows(occ_rows, occupied_decay)
    vir_rows = scale_rows(vir_rows, virtual_decay)
    green_occ = lax.dot_general(plane_occ, occ_rows, contract, preferred_element_type=jnp.float32)
    green_vir = lax.dot_general(plane_vir, vir_rows, contract, preferred_element_type=jnp.float32)
    polar = green_occ * green_vir * factor
    cube = polar.reshape(1, NB, NC, row_count * sub_rows)
    real_part, imag_part = real_step(cube, "abcr,cw->wabr", NC)
    real_part, imag_part = complex_step(real_part, imag_part, "wabr,bv->wavr", NB)
    blocked = (NC, 1, NB, row_count, sub_rows)
    real_part, imag_part = (
        lax.all_to_all(
            lax.all_to_all(
                real_part.reshape(blocked), "row", split_axis=3, concat_axis=3, tiled=True
            ),
            "col",
            split_axis=0,
            concat_axis=1,
            tiled=True,
        ),
        lax.all_to_all(
            lax.all_to_all(
                imag_part.reshape(blocked), "row", split_axis=3, concat_axis=3, tiled=True
            ),
            "col",
            split_axis=0,
            concat_axis=1,
            tiled=True,
        ),
    )

    def settle(part):
        kc_share = part.shape[0]
        part = part.reshape(kc_share, part.shape[1], NB, per_col, spread, sub_rows)
        part = jnp.transpose(part, (0, 1, 3, 2, 4, 5))
        return part.reshape(kc_share, NA, NB, ROWS_DEV)

    real_part, imag_part = complex_step(settle(real_part), settle(imag_part), "wavr,au->rwuv", NA)
    normal = 1.0 / math.sqrt(NGRID)
    final_shape = (real_part.shape[0], real_part.shape[1], NA * NB)
    return ((real_part * normal).reshape(final_shape), (imag_part * normal).reshape(final_shape))


def solution(mesh):
    in_specs = (P("row", "col"), P("row", "col"), P(), P())
    out_specs = (P("row", "col", None), P("row", "col", None))
    return jax.shard_map(
        on_device, mesh=mesh, in_specs=in_specs, out_specs=out_specs, check_vma=False
    )
```

profile of v0, /device:TPU:0, one launch (start us, length us, event | category | flops | bytes accessed | tf_op | source)
XLA Modules:
  0.0 502.8 jit_solution(10017124884010591523)
XLA Ops:
  9.4 7.4 %all-to-all-start.2 = ((bf16[32,16,512]{2,0,1:T(8,128)(2,1)}), bf16[32,16,512]{2,0,1:T(8,128)(2,1)S(1)}, u32[]{:S(2)}, u32[]{:S(2)}) async-start(bf16[32,16,512]{2,0,1:T(8,128)(2,1)} %broadcast_in_dim.11), calls=%async_computation.2 | async-start | bytes 1048576 | tf_op jit(solution)/shard_map/all_to_all | solution.py:86
  17.3 13.9 %all-to-all-done.2 = bf16[32,16,512]{2,0,1:T(8,128)(2,1)S(1)} async-done(((bf16[32,16,512]{2,0,1:T(8,128)(2,1)}), bf16[32,16,512]{2,0,1:T(8,128)(2,1)S(1)}, u32[]{:S(2)}, u32[]{:S(2)}) %all-to-all-start.2) | async-done | bytes 524320 | tf_op jit(solution)/shard_map/all_to_all | solution.py:86
  32.3 4.2 all-to-all-start
  38.0 21.3 %all-to-all-done = bf16[64,16,512]{2,0,1:T(8,128)(2,1)S(1)} async-done(((bf16[64,16,512]{2,0,1:T(8,128)(2,1)}), bf16[64,16,512]{2,0,1:T(8,128)(2,1)S(1)}, u32[]{:S(2)}, u32[]{:S(2)}) %all-to-all-start) | async-done | bytes 1048608 | tf_op jit(solution)/shard_map/all_to_all | solution.py:85
  60.3 6.9 %all-to-all-start.1 = ((bf16[64,16,1024]{2,0,1:T(8,128)(2,1)}), bf16[64,16,1024]{2,0,1:T(8,128)(2,1)S(1)}, u32[]{:S(2)}, u32[]{:S(2)}) async-start(bf16[64,16,1024]{2,0,1:T(8,128)(2,1)} %bitcast.123), calls=%async_computation.1 | async-start | bytes 4194304 | tf_op jit(solution)/shard_map/all_to_all | solution.py:77
  68.3 39.9 %all-to-all-done.1 = bf16[64,16,1024]{2,0,1:T(8,128)(2,1)S(1)} async-done(((bf16[64,16,1024]{2,0,1:T(8,128)(2,1)}), bf16[64,16,1024]{2,0,1:T(8,128)(2,1)S(1)}, u32[]{:S(2)}, u32[]{:S(2)}) %all-to-all-start.1) | async-done | bytes 2097184 | tf_op jit(solution)/shard_map/all_to_all | solution.py:77
  108.2 11.2 %all-to-all-start.3 = ((bf16[32,16,1024]{2,0,1:T(8,128)(2,1)}), bf16[32,16,1024]{2,0,1:T(8,128)(2,1)S(1)}, u32[]{:S(2)}, u32[]{:S(2)}) async-start(bf16[32,16,1024]{2,0,1:T(8,128)(2,1)} %bitcast.126), calls=%async_computation.3 | async-start | bytes 2097152 | tf_op jit(solution)/shard_map/all_to_all | solution.py:80
  120.2 56.0 %all-reduce.3.cloned.1.call-done = (bf16[1024,512]{1,0:T(8,128)(2,1)}, bf16[512,512]{1,0:T(8,128)(2,1)}) async-done(((bf16[1024,512]{1,0:T(8,128)(2,1)}, bf16[512,512]{1,0:T(8,128)(2,1)}), (bf16[1024,512]{1,0:T(8,128)(2,1)}, bf16[512,512]{1,0:T(8,128)(2,1)})) %all-reduce.3.cloned.1.call-update) | async-done | bytes 1572880 | tf_op jit(solution)/shard_map/psum | solution.py:89
  176.1 3.9 fusion.12
  180.0 3.9 multiply_bitcast_fusion.2
  189.3 4.3 fusion.29
  196.6 4.4 subtract_bitcast_fusion
  201.0 6.4 %reshape.86 = f32[32,1,32,16,32]{4,3,2,0,1:T(8,128)} reshape(f32[32,1,32,512]{3,2,0,1:T(8,128)} %subtract_bitcast_fusion) | data formatting | bytes 4194304 | tf_op jit(solution)/shard_map/reshape | solution.py:113
  207.4 9.3 %copy.71 = f32[32,1,32,16,32]{4,2,0,1,3:T(8,128)} copy(f32[32,1,32,16,32]{4,3,2,0,1:T(8,128)} %reshape.86) | data formatting | bytes 4194304 | tf_op jit(solution)/shard_map/reshape | solution.py:113
  216.7 8.6 %reshape.99 = f32[16,1,32768]{2,1,0:T(1,128)} reshape(f32[16,1,32,32,32]{4,3,2,1,0:T(8,128)} %bitcast.113) | data formatting | bytes 4194304
  225.3 5.7 %all-to-all-start.6 = ((f32[16,1,32768]{2,1,0:T(1,128)}), f32[16,1,32768]{2,1,0:T(1,128)}, u32[]{:S(2)}, u32[]{:S(2)}) async-start(f32[16,1,32768]{2,1,0:T(1,128)} %reshape.99), calls=%async_computation.6 | async-start | bytes 4194304 | tf_op jit(solution)/shard_map/all_to_all | solution.py:112
  230.9 4.6 fusion.2
  235.5 4.4 add_bitcast_fusion
  239.9 6.2 %reshape.83 = f32[32,1,32,16,32]{4,3,2,0,1:T(8,128)} reshape(f32[32,1,32,512]{3,2,0,1:T(8,128)} %add_bitcast_fusion) | data formatting | bytes 4194304 | tf_op jit(solution)/shard_map/reshape | solution.py:104
  246.1 9.3 %copy.72 = f32[32,1,32,16,32]{4,2,0,1,3:T(8,128)} copy(f32[32,1,32,16,32]{4,3,2,0,1:T(8,128)} %reshape.83) | data formatting | bytes 4194304 | tf_op jit(solution)/shard_map/reshape | solution.py:104
  255.4 8.6 %reshape.95 = f32[16,1,32768]{2,1,0:T(1,128)} reshape(f32[16,1,32,32,32]{4,3,2,1,0:T(8,128)} %bitcast.114) | data formatting | bytes 4194304
  263.9 8.0 %all-to-all-done.6 = f32[16,1,32768]{2,1,0:T(1,128)} async-done(((f32[16,1,32768]{2,1,0:T(1,128)}), f32[16,1,32768]{2,1,0:T(1,128)}, u32[]{:S(2)}, u32[]{:S(2)}) %all-to-all-start.6) | async-done | bytes 2097184 | tf_op jit(solution)/shard_map/all_to_all | solution.py:112
  272.0 11.7 %all-to-all-start.4 = ((f32[16,1,32768]{2,1,0:T(1,128)}), f32[16,1,32768]{2,1,0:T(1,128)}, u32[]{:S(2)}, u32[]{:S(2)}) async-start(f32[16,1,32768]{2,1,0:T(1,128)} %reshape.95), calls=%async_computation.4 | async-start | bytes 4194304 | tf_op jit(solution)/shard_map/all_to_all | solution.py:103
  284.2 7.3 %reduce.2 = f32[16,32768]{1,0:T(8,128)S(1)} reduce(f32[16,1,32768]{2,1,0:T(1,128)} %all-to-all-done.6, f32[]{:T(128)} %broadcast.102), dimensions={1}, to_apply=%all_to_all.98.reduce_sub_computation | reduce | bytes 4194308 | tf_op jit(solution)/shard_map/all_to_all | solution.py:112
  291.5 4.9 reshape.100
  296.4 14.2 %copy.45 = f32[32,1,32,16,32]{4,3,2,1,0:T(8,128)} copy(f32[32,1,32,16,32]{4,2,0,1,3:T(8,128)} %bitcast.115) | data formatting | bytes 4194304 | tf_op jit(solution)/shard_map/all_to_all | solution.py:112
  310.6 6.8 %reshape.101 = f32[2,1,262144]{2,1,0:T(1,128)} reshape(f32[32,1,32,16,32]{4,3,2,1,0:T(8,128)} %copy.45) | data formatting | bytes 4194304
  317.4 7.2 %all-to-all-done.4 = f32[16,1,32768]{2,1,0:T(1,128)} async-done(((f32[16,1,32768]{2,1,0:T(1,128)}), f32[16,1,32768]{2,1,0:T(1,128)}, u32[]{:S(2)}, u32[]{:S(2)}) %all-to-all-start.4) | async-done | bytes 2097184 | tf_op jit(solution)/shard_map/all_to_all | solution.py:103
  324.7 5.0 all-to-all-start.7
  329.7 7.3 %reduce = f32[16,32768]{1,0:T(8,128)S(1)} reduce(f32[16,1,32768]{2,1,0:T(1,128)} %all-to-all-done.4, f32[]{:T(128)} %broadcast.102), dimensions={1}, to_apply=%all_to_all.94.reduce_sub_computation | reduce | bytes 4194308 | tf_op jit(solution)/shard_map/all_to_all | solution.py:103
  337.0 4.8 reshape.96
  341.7 14.2 %copy.40 = f32[32,1,32,16,32]{4,3,2,1,0:T(8,128)} copy(f32[32,1,32,16,32]{4,2,0,1,3:T(8,128)} %bitcast.116) | data formatting | bytes 4194304 | tf_op jit(solution)/shard_map/all_to_all | solution.py:103
  355.9 6.8 %reshape.97 = f32[2,1,262144]{2,1,0:T(1,128)} reshape(f32[32,1,32,16,32]{4,3,2,1,0:T(8,128)} %copy.40) | data formatting | bytes 4194304
  362.7 4.8 all-to-all-start.5
  367.6 8.5 %reduce.3 = f32[2,262144]{1,0:T(2,128)S(1)} reduce(f32[2,1,262144]{2,1,0:T(1,128)} %all-to-all-done.7, f32[]{:T(128)} %broadcast.102), dimensions={1}, to_apply=%all_to_all.99.reduce_sub_computation | reduce | bytes 4194308 | tf_op jit(solution)/shard_map/all_to_all | solution.py:111
  376.1 6.4 %reshape.102 = f32[32,1,32,16,32]{4,3,2,1,0:T(8,128)} reshape(f32[2,262144]{1,0:T(2,128)S(1)} %reduce.3) | data formatting | bytes 4194304
  382.5 7.7 %copy.46 = f32[2,16,1,32,16,32]{5,4,0,3,1,2:T(8,128)} copy(f32[2,16,1,32,16,32]{5,4,3,1,0,2:T(8,128)} %bitcast.117) | data formatting | bytes 4194304 | tf_op jit(solution)/shard_map/all_to_all | solution.py:111
  393.9 8.2 %reduce.1 = f32[2,262144]{1,0:T(2,128)S(1)} reduce(f32[2,1,262144]{2,1,0:T(1,128)} %all-to-all-done.5, f32[]{:T(128)} %broadcast.102), dimensions={1}, to_apply=%all_to_all.95.reduce_sub_computation | reduce | bytes 4194308 | tf_op jit(solution)/shard_map/all_to_all | solution.py:102
  402.2 6.4 %reshape.98 = f32[32,1,32,16,32]{4,3,2,1,0:T(8,128)} reshape(f32[2,262144]{1,0:T(2,128)S(1)} %reduce.1) | data formatting | bytes 4194304
  408.6 4.6 copy.41
  413.2 9.5 %fusion.22 = f32[32,16,32,32]{3,0,2,1:T(8,128)} fusion(f32[16,32,32,32]{3,1,2,0:T(8,128)S(1)} %bitcast.111), kind=kOutput, calls=%fused_computation.31 | convolution fusion | flops 201340928 | bytes 4194304 | tf_op jit(solution)/shard_map/wavr,au->rwuv/dot_general | solution.py:25
  422.7 9.8 %fusion.20 = f32[32,16,32,32]{3,0,2,1:T(8,128)} fusion(f32[16,32,32,32]{3,1,2,0:T(8,128)S(1)} %bitcast.109), kind=kOutput, calls=%fused_computation.29 | convolution fusion | flops 201340928 | bytes 4194304 | tf_op jit(solution)/shard_map/wavr,au->rwuv/dot_general | solution.py:25
  432.5 12.1 %multiply_bitcast_fusion.1 = f32[32,16,32,32]{0,2,3,1:T(8,128)} fusion(f32[32,16,32,32]{3,0,2,1:T(8,128)} %fusion.22, f32[16,32,32,32]{3,1,2,0:T(8,128)S(1)} %bitcast.110), kind=kOutput, calls=%fused_computation.1 | convolution fusion | flops 202389504 | bytes 6291456 | tf_op jit(solution)/shard_map/wavr,au->rwuv/dot_general | solution.py:25
  444.6 12.4 %multiply_bitcast_fusion = f32[32,16,32,32]{0,2,3,1:T(8,128)} fusion(f32[32,16,32,32]{3,0,2,1:T(8,128)} %fusion.20, f32[16,32,32,32]{3,1,2,0:T(8,128)S(1)} %bitcast.112), kind=kOutput, calls=%fused_computation | convolution fusion | flops 202389504 | bytes 6291456 | tf_op jit(solution)/shard_map/wavr,au->rwuv/dot_general | solution.py:25
  457.0 11.7 %copy.48 = f32[32,16,32,32]{3,2,1,0:T(8,128)} copy(f32[32,16,32,32]{0,2,3,1:T(8,128)} %multiply_bitcast_fusion) | data formatting | bytes 4194304 | tf_op jit(solution)/shard_map/mul | solution.py:131
  468.7 7.7 %reshape.90 = f32[32,16,1024]{2,1,0:T(8,128)} reshape(f32[32,16,32,32]{3,2,1,0:T(8,128)} %copy.48) | data formatting | bytes 4194304 | tf_op jit(solution)/shard_map/reshape | solution.py:131
  476.4 11.7 %copy.47 = f32[32,16,32,32]{3,2,1,0:T(8,128)} copy(f32[32,16,32,32]{0,2,3,1:T(8,128)} %multiply_bitcast_fusion.1) | data formatting | bytes 4194304 | tf_op jit(solution)/shard_map/mul | solution.py:131
  488.0 7.7 %reshape.89 = f32[32,16,1024]{2,1,0:T(8,128)} reshape(f32[32,16,32,32]{3,2,1,0:T(8,128)} %copy.47) | data formatting | bytes 4194304 | tf_op jit(solution)/shard_map/reshape | solution.py:131
  (40 shorter events, 20.7 us)
Async XLA Ops:
  8.6 8.4 %copy-start.2 = (bf16[64,16384]{1,0:T(8,128)(2,1)S(1)}, bf16[64,16384]{1,0:T(8,128)(2,1)}, u32[]{:S(2)}) copy-start(bf16[64,16384]{1,0:T(8,128)(2,1)} %param.4) | copy-start | bytes 6291460
  9.4 21.7 %all-to-all-start.2 = ((bf16[32,16,512]{2,0,1:T(8,128)(2,1)}), bf16[32,16,512]{2,0,1:T(8,128)(2,1)S(1)}, u32[]{:S(2)}, u32[]{:S(2)}) async-start(bf16[32,16,512]{2,0,1:T(8,128)(2,1)} %broadcast_in_dim.11), calls=%async_computation.2 | async-start | bytes 1048576 | tf_op jit(solution)/shard_map/all_to_all | solution.py:86
  31.1 1.1 copy-start.5
  32.3 27.1 %all-to-all-start = ((bf16[64,16,512]{2,0,1:T(8,128)(2,1)}), bf16[64,16,512]{2,0,1:T(8,128)(2,1)S(1)}, u32[]{:S(2)}, u32[]{:S(2)}) async-start(bf16[64,16,512]{2,0,1:T(8,128)(2,1)} %broadcast_in_dim.9), calls=%async_computation | async-start | bytes 2097152 | tf_op jit(solution)/shard_map/all_to_all | solution.py:85
  59.3 1.0 copy-start.4
  60.3 6.9 %copy-start.3 = (bf16[32,16384]{1,0:T(8,128)(2,1)S(1)}, bf16[32,16384]{1,0:T(8,128)(2,1)}, u32[]{:S(2)}) copy-start(bf16[32,16384]{1,0:T(8,128)(2,1)} %param.5) | copy-start | bytes 3145732
  60.3 47.9 %all-to-all-start.1 = ((bf16[64,16,1024]{2,0,1:T(8,128)(2,1)}), bf16[64,16,1024]{2,0,1:T(8,128)(2,1)S(1)}, u32[]{:S(2)}, u32[]{:S(2)}) async-start(bf16[64,16,1024]{2,0,1:T(8,128)(2,1)} %bitcast.123), calls=%async_computation.1 | async-start | bytes 4194304 | tf_op jit(solution)/shard_map/all_to_all | solution.py:77
  68.3 107.8 %copy-start.6 = (f32[1024]{0:T(1024)S(1)}, f32[1024]{0:T(1024)}, u32[]{:S(2)}) copy-start(f32[1024]{0:T(1024)} %param.6) | copy-start | bytes 12292
  108.2 71.8 %all-to-all-start.3 = ((bf16[32,16,1024]{2,0,1:T(8,128)(2,1)}), bf16[32,16,1024]{2,0,1:T(8,128)(2,1)S(1)}, u32[]{:S(2)}, u32[]{:S(2)}) async-start(bf16[32,16,1024]{2,0,1:T(8,128)(2,1)} %bitcast.126), calls=%async_computation.3 | async-start | bytes 2097152 | tf_op jit(solution)/shard_map/all_to_all | solution.py:80
  119.4 56.7 %all-reduce.3.cloned.1.call-start = ((), (), s32[]{:S(2)}) async-start(), calls=%async_computation.8 | async-start | bytes 3145728 | tf_op jit(solution)/shard_map/psum | solution.py:89
  176.1 3.9 copy-start.7
  186.0 1.3 copy-start.1
  189.3 4.3 copy-start
  225.3 46.7 %all-to-all-start.6 = ((f32[16,1,32768]{2,1,0:T(1,128)}), f32[16,1,32768]{2,1,0:T(1,128)}, u32[]{:S(2)}, u32[]{:S(2)}) async-start(f32[16,1,32768]{2,1,0:T(1,128)} %reshape.99), calls=%async_computation.6 | async-start | bytes 4194304 | tf_op jit(solution)/shard_map/all_to_all | solution.py:112
  272.0 52.7 %all-to-all-start.4 = ((f32[16,1,32768]{2,1,0:T(1,128)}), f32[16,1,32768]{2,1,0:T(1,128)}, u32[]{:S(2)}, u32[]{:S(2)}) async-start(f32[16,1,32768]{2,1,0:T(1,128)} %reshape.95), calls=%async_computation.4 | async-start | bytes 4194304 | tf_op jit(solution)/shard_map/all_to_all | solution.py:103
  324.7 38.1 %all-to-all-start.7 = ((f32[2,1,262144]{2,1,0:T(1,128)}), f32[2,1,262144]{2,1,0:T(1,128)}, u32[]{:S(2)}, u32[]{:S(2)}) async-start(f32[2,1,262144]{2,1,0:T(1,128)} %reshape.101), calls=%async_computation.7 | async-start | bytes 4194304 | tf_op jit(solution)/shard_map/all_to_all | solution.py:111
  362.7 31.2 %all-to-all-start.5 = ((f32[2,1,262144]{2,1,0:T(1,128)}), f32[2,1,262144]{2,1,0:T(1,128)}, u32[]{:S(2)}, u32[]{:S(2)}) async-start(f32[2,1,262144]{2,1,0:T(1,128)} %reshape.97), calls=%async_computation.5 | async-start | bytes 4194304 | tf_op jit(solution)/shard_map/all_to_all | solution.py:102
  408.6 14.1 %slice-start = ((s8[8388608]{0:T(1024)(128)(4,1)}), s8[4194304]{0:T(1024)(128)(4,1)S(1)}, s32[]{:S(2)}) async-start(s8[8388608]{0:T(1024)(128)(4,1)} %bitcast.107), calls=%async_computation.9 | async-start | bytes 8388608
  413.2 9.5 %slice-start.1 = ((s8[8388608]{0:T(1024)(128)(4,1)}), s8[4194304]{0:T(1024)(128)(4,1)S(1)}, s32[]{:S(2)}) async-start(s8[8388608]{0:T(1024)(128)(4,1)} %bitcast.107), calls=%async_computation.10 | async-start | bytes 8388608
Sparse Core Ops, SparseCore 0:
  123.2 52.8 all-reduce.2
where the time goes:
time: 513 us; the launch traced here: 503 us
  local copies, waits for them, and re-layouts  175 us (34%)
  waiting for transfers between devices  151 us (29%)
  matrix products  74.2 us (14%)
  starting transfers between devices  56.9 us (11%)
  other arithmetic  31.2 us (6%)
  between operations  14.6 us (3%)
    dot_general x10, matrix products, apply_table(): return jnp.einsum(form, data, table, precision=lax.Precision.HIGHEST)  66.3 us
    psum x1, waiting for transfers between devices, on_device(): lax.psum(part_occ.astype(jnp.float32).astype(jnp.bfloat16), 'col')  56 us
    unnamed x28, local copies, waits for them, and re-layouts  55.6 us
    all_to_all x1, waiting for transfers between devices, on_device(): lax.all_to_all(spread_planes(occupied_waves), 'row', split_axis=1, concat...  39.9 us
    all_to_all x1, waiting for transfers between devices, on_device(): lax.all_to_all(pick_rows(occupied_waves), 'row', split_axis=1, concat_axi...  21.3 us
    reshape x2, local copies, waits for them, and re-layouts, on_device(): imag_part.reshape(blocked)  15.7 us
    reshape x2, local copies, waits for them, and re-layouts, on_device(): real_part.reshape(blocked)  15.5 us
    all_to_all x2, local copies, waits for them, and re-layouts, on_device(): lax.all_to_all(real_part.reshape(blocked), 'row', split_axis=3, concat_ax...  14.8 us
  transfers between devices with their start and end apart: 9, of which 7 were waited for; matrix products, arithmetic and copies ran while one was open for 26% of the time, Pallas kernels for 0%

commit v1 on v0

v1 whole, which is shorter than its diff:
```python
import functools
import math

import jax
import jax.numpy as jnp
import numpy as np
from jax import lax
from jax.experimental import pallas as pl
from jax.experimental.pallas import tpu as pltpu
from jax.sharding import PartitionSpec as P

NA = 32
NB = 32
NC = 32
NAB = NA * NB
NGRID = NA * NB * NC
LANES = 128
R_BLOCK = 16


def trig(phase, length):
    angle = (phase % length) * (2.0 * math.pi / length)
    return np.cos(angle), np.sin(angle)


def bf16_table(table):
    return jnp.asarray(table.astype(np.float32)).astype(jnp.bfloat16)


def plane_tables():
    index = np.arange(NAB)
    a, b = index // NB, index % NB
    phase = a[:, None] * a[None, :] * NB + b[:, None] * b[None, :] * NA
    cosine, sine = trig(phase, NA * NB)
    return bf16_table(cosine), bf16_table(sine)


def line_tables(col_count):
    share = NC // col_count
    full = np.zeros((col_count, 2, R_BLOCK, share, NC, R_BLOCK))
    for y in range(col_count):
        kc = y * share + np.arange(share)
        cosine, sine = trig(kc[:, None] * np.arange(NC)[None, :], NC)
        for r in range(R_BLOCK):
            full[y, 0, r, :, :, r] = cosine
            full[y, 1, r, :, :, r] = -sine
    return bf16_table(full.reshape(col_count, 2 * R_BLOCK * share, NC * R_BLOCK))


def swap_table(outer, inner, width):
    index = np.arange(outer * inner * width).reshape(outer, inner, width)
    source = np.transpose(index, (1, 0, 2)).reshape(-1)
    table = np.zeros((source.size, source.size))
    table[source, np.arange(source.size)] = 1.0
    return bf16_table(table)


def dot(a, b):
    return jnp.dot(a, b, preferred_element_type=jnp.float32)


def spectrum_kernel(pieces, x_ref, swap_ref, line_ref, cos_ref, sin_ref, re_ref, im_ref, rows):
    if pieces:
        per = LANES // NB
        for g in range(NA // per):
            parts = []
            for t in range(NC // per):
                lanes = pl.ds(t * LANES, LANES)
                parts.append(
                    jnp.concatenate([x_ref[g * per + k, :, lanes] for k in range(per)], axis=1)
                )
            moved = dot(jnp.concatenate(parts, axis=0), swap_ref[...]).astype(jnp.bfloat16)
            for t in range(NC // per):
                for j in range(per):
                    rows[pl.ds((t * per + j) * R_BLOCK, R_BLOCK), pl.ds(g * LANES, LANES)] = moved[
                        t * R_BLOCK : (t + 1) * R_BLOCK, j * LANES : (j + 1) * LANES
                    ]
    else:
        rows[...] = x_ref[...].reshape(NC * R_BLOCK, NAB)
    line = dot(line_ref[...], rows[...]).astype(jnp.bfloat16)
    half = line.shape[0] // 2
    re, im = line[:half], line[half:]
    re_ref[...] = dot(re, cos_ref[...]) + dot(im, sin_ref[...])
    im_ref[...] = dot(im, cos_ref[...]) - dot(re, sin_ref[...])


def spectrum(pieces, x, line_table):
    r_count = x.shape[1]
    cosine, sine = plane_tables()
    per = LANES // NB
    swap = swap_table(per, per, NB)
    out_rows = line_table.shape[0] // 2
    steps = r_count // R_BLOCK
    whole = lambda table: pl.BlockSpec(table.shape, lambda i: (0, 0))
    out = jax.ShapeDtypeStruct((out_rows * steps, NAB), jnp.float32)
    out_spec = pl.BlockSpec((out_rows, NAB), lambda i: (i, 0))
    return pl.pallas_call(
        functools.partial(spectrum_kernel, pieces),
        grid=(steps,),
        in_specs=[
            pl.BlockSpec((x.shape[0], R_BLOCK, x.shape[2]), lambda i: (0, i, 0)),
            whole(swap),
            whole(line_table),
            whole(cosine),
            whole(sine),
        ],
        out_specs=[out_spec, out_spec],
        out_shape=[out, out],
        scratch_shapes=[pltpu.VMEM((NC * R_BLOCK, NAB), jnp.bfloat16)],
        compiler_params=pltpu.CompilerParams(vmem_limit_bytes=48 * 1024 * 1024),
    )(x, swap, line_table, cosine, sine)


def on_device(rows_dev, occupied_waves, virtual_waves, occupied_decay, virtual_decay):
    row_count = lax.axis_size("row")
    col_count = lax.axis_size("col")
    occ_share = occupied_waves.shape[0]
    share = occ_share + virtual_waves.shape[0]
    nocc, nvir = occupied_decay.shape[0], virtual_decay.shape[0]
    window = rows_dev * row_count
    points = occupied_waves.shape[1] // row_count
    contract = (((0,), (0,)), ((), ()))
    factor = -1.0 / math.sqrt(nocc * nvir) / math.sqrt(NGRID)

    first = jnp.concatenate([occupied_waves[:, :window], virtual_waves[:, :window]], axis=0)
    first = lax.all_gather(first, "col")[0]
    first = lax.all_gather(first, "row")

    def exchange(waves):
        shaped = waves.reshape(waves.shape[0], row_count, points)
        shaped = lax.all_to_all(shaped, "row", split_axis=1, concat_axis=0, tiled=True)
        return shaped.reshape(waves.shape[0] * row_count, points)

    plane_occ = exchange(occupied_waves)
    plane_vir = exchange(virtual_waves)

    def scaled(rows, decay):
        rows = rows.reshape(decay.shape[0], window).astype(jnp.float32)
        return (rows * decay[:, None]).astype(jnp.bfloat16)

    occ_rows = scaled(first[:, :occ_share], occupied_decay)
    vir_rows = scaled(first[:, occ_share:], virtual_decay)
    green_occ = lax.dot_general(occ_rows, plane_occ, contract, preferred_element_type=jnp.float32)
    green_vir = lax.dot_general(vir_rows, plane_vir, contract, preferred_element_type=jnp.float32)
    polar = (green_occ * green_vir * factor).astype(jnp.bfloat16)
    polar = dot(polar, swap_table(points // NC, NC, 1)).astype(jnp.bfloat16)
    polar = polar.reshape(row_count, rows_dev, points)
    polar = lax.all_to_all(polar, "row", split_axis=0, concat_axis=0, tiled=True)
    polar = lax.all_gather(polar, "col")
    pieces = points == NB * NC
    if pieces:
        x = polar.reshape(col_count * row_count, rows_dev, points)
    else:
        x = polar.reshape(col_count * row_count, rows_dev, NC, points // NC)
        x = jnp.transpose(x, (2, 1, 0, 3)).reshape(NC, rows_dev, NAB)
    table = lax.dynamic_index_in_dim(line_tables(col_count), lax.axis_index("col"), 0, False)
    real_part, imag_part = spectrum(pieces, x, table)
    shape = (rows_dev, NC // col_count, NAB)
    return real_part.reshape(shape), imag_part.reshape(shape)


ROWS_DEV = 32


def solution(mesh):
    in_specs = (P("row", "col"), P("row", "col"), P(), P())
    out_specs = (P("row", "col", None), P("row", "col", None))
    return jax.shard_map(
        functools.partial(on_device, ROWS_DEV),
        mesh=mesh,
        in_specs=in_specs,
        out_specs=out_specs,
        check_vma=False,
    )
```

time: 513 us -> 191 us (0.37); the launches traced: 503 us -> 191 us
  local copies, waits for them, and re-layouts: 175 us -> 8.56 us
  matrix products: 74.2 us -> 7.79 us
  waiting for transfers between devices: 151 us -> 84.7 us
  blocking collectives: 0 us -> 37.6 us
  starting transfers between devices: 56.9 us -> 24.6 us
  other arithmetic: 31.2 us -> 3.56 us
  Pallas kernels: 0 us -> 9.66 us
    dot_general x12 -> x2, matrix products: 74.2 us -> 7.79 us  [the longest x1 5.17 us: dot(): return jnp.dot(a, b, preferred_element_type=jnp.float32)]
    psum x1 -> x0, waiting for transfers between devices: 56 us -> none  [on_device(): lax.psum(part_occ.astype(jnp.float32).astype(jnp.bfloat16), 'col')]
    unnamed x28 -> x12, local copies, waits for them, and re-layouts: 55.6 us -> 1.62 us
    all_to_all x7 -> x0, local copies, waits for them, and re-layouts: 43.9 us -> none  [the longest x2 14.8 us: on_device(): lax.all_to_all(real_part.reshape(blocked), 'row', split_axis=3, concat_ax...]
    reshape x6 -> x2, local copies, waits for them, and re-layouts: 46.6 us -> 4.22 us  [exchange(): shaped = waves.reshape(waves.shape[0], row_count, points)]
    all_to_all x8 -> x2, waiting for transfers between devices: 94 us -> 52.2 us  [exchange(): lax.all_to_all(shaped, 'row', split_axis=1, concat_axis=0, tiled=True)]
    all_gather x0 -> x2, waiting for transfers between devices: none -> 32.5 us  [the longest x1 32.5 us: on_device(): polar = lax.all_gather(polar, 'col')]
    all_to_all x8 -> x2, starting transfers between devices: 56.9 us -> 24.6 us  [exchange(): lax.all_to_all(shaped, 'row', split_axis=1, concat_axis=0, tiled=True)]
  transfers between devices with their start and end apart: 9 -> 4, of which waited for: 7 -> 3; matrix products, arithmetic and copies ran while one was open for 26% -> 5% of each run, Pallas kernels for 0% -> 0%
where the time goes in v1:
time: 191 us
  waiting for transfers between devices  84.7 us (44%)
  blocking collectives  37.6 us (20%)
  starting transfers between devices  24.6 us (13%)
  between operations  14.1 us (7%)
  Pallas kernels  9.66 us (5%)
  local copies, waits for them, and re-layouts  8.56 us (4%)
  matrix products  7.79 us (4%)
  other arithmetic  3.56 us (2%)
    all_to_all x2, waiting for transfers between devices, exchange(): lax.all_to_all(shaped, 'row', split_axis=1, concat_axis=0, tiled=True)  52.2 us
    all_gather x1, waiting for transfers between devices, on_device(): polar = lax.all_gather(polar, 'col')  32.5 us
    all_to_all x1, blocking collectives, on_device(): lax.all_to_all(polar, 'row', split_axis=0, concat_axis=0, tiled=True)  31.8 us
    all_to_all x2, starting transfers between devices, exchange(): lax.all_to_all(shaped, 'row', split_axis=1, concat_axis=0, tiled=True)  24.6 us
    pallas_call x1, Pallas kernels, spectrum(): pl.pallas_call(functools.partial(spectrum_kernel, pieces), grid=(steps,),...  9.66 us
    all_gather x1, blocking collectives, on_device(): first = lax.all_gather(first, 'col')[0]  5.77 us
    dot_general x1, matrix products, dot(): return jnp.dot(a, b, preferred_element_type=jnp.float32)  5.17 us
    reshape x2, local copies, waits for them, and re-layouts, exchange(): shaped = waves.reshape(waves.shape[0], row_count, points)  4.22 us
  transfers between devices with their start and end apart: 4, of which 3 were waited for; matrix products, arithmetic and copies ran while one was open for 5% of the time, Pallas kernels for 0%

profile of v1, /device:TPU:0, one launch (start us, length us, event | category | flops | bytes accessed | tf_op | source)
XLA Modules:
  0.0 190.7 jit_solution(13261362766991942485)
XLA Ops:
  7.2 3.2 %copy.19 = bf16[8,16,8,1024]{3,2,0,1:T(8,128)(2,1)} copy(bf16[8,16,8,1024]{3,2,1,0:T(8,128)(2,1)} %bitcast.34) | data formatting | bytes 4194304 | tf_op jit(solution)/shard_map/reshape | solution.py:130
  10.3 0.0 slice-start
  10.3 0.0 copy-start.3
  10.3 7.5 %all-to-all-start = ((bf16[64,16,1024]{2,0,1:T(8,128)(2,1)}), bf16[64,16,1024]{2,0,1:T(8,128)(2,1)S(1)}, u32[]{:S(2)}, u32[]{:S(2)}) async-start(bf16[64,16,1024]{2,0,1:T(8,128)(2,1)} %bitcast.32), calls=%async_computation | async-start | bytes 4194304 | tf_op jit(solution)/shard_map/all_to_all | solution.py:131
  17.8 0.0 all-gather.8.cloned.1.call-start
  17.9 0.8 slice.15
  18.7 0.0 slice-done
  18.8 5.8 %all-gather = bf16[192,512]{1,0:T(8,128)(2,1)S(1)} all-gather(bf16[96,512]{1,0:T(8,128)(2,1)S(1)} %pad_maximum_fusion), channel_id=2, replica_groups=mesh['row'=16,'col'=2] {'col'}, dimensions={0}, use_global_device_ids=true | all-gather | bytes 294912 | tf_op jit(solution)/shard_map/all_gather | solution.py:126
  24.5 0.6 slice.21
  25.2 0.0 all-gather.8.cloned.1.call-update
  25.2 0.0 copy-done.3
  25.2 0.0 copy-start.4
  25.2 0.0 copy-start.5
  25.2 1.1 copy.20
  26.3 35.7 %all-to-all-done = bf16[64,16,1024]{2,0,1:T(8,128)(2,1)S(1)} async-done(((bf16[64,16,1024]{2,0,1:T(8,128)(2,1)}), bf16[64,16,1024]{2,0,1:T(8,128)(2,1)S(1)}, u32[]{:S(2)}, u32[]{:S(2)}) %all-to-all-start) | async-done | bytes 2097184 | tf_op jit(solution)/shard_map/all_to_all | solution.py:131
  62.0 17.0 %all-to-all-start.1 = ((bf16[32,16,1024]{2,0,1:T(8,128)(2,1)}), bf16[32,16,1024]{2,0,1:T(8,128)(2,1)S(1)}, u32[]{:S(2)}, u32[]{:S(2)}) async-start(bf16[32,16,1024]{2,0,1:T(8,128)(2,1)} %bitcast.30), calls=%async_computation.1 | async-start | bytes 2097152 | tf_op jit(solution)/shard_map/all_to_all | solution.py:131
  79.0 0.0 all-gather.6.cloned.1.call-start
  79.1 0.0 copy-done.4
  79.1 0.1 mul.31
  79.2 0.0 copy-done.5
  79.2 0.1 mul.34
  79.2 0.0 all-gather.8.cloned.1.call-done
  79.2 2.0 %multiply_convert_fusion.2 = bf16[16,32,512]{2,1,0:T(8,128)(2,1)} fusion(bf16[16,96,512]{2,1,0:T(8,128)(2,1)} %bitcast.35, f32[16,32]{1,0:T(8,128)S(1)} %mul.34), kind=kLoop, calls=%fused_computation.5 | loop fusion | flops 786432 | bytes 1050624 | tf_op jit(solution)/shard_map/convert_element_type | solution.py:139
  81.3 1.5 multiply_convert_fusion.1
  82.8 2.6 %fusion.1 = f32[512,1024]{1,0:T(8,128)} fusion(bf16[1024,512]{1,0:T(8,128)(2,1)S(1)} %bitcast.33, bf16[1024,1024]{1,0:T(8,128)(2,1)S(1)} %bitcast.31), kind=kOutput, calls=%fused_computation.9 | convolution fusion | flops 1073741824 | bytes 5242880 | tf_op jit(solution)/shard_map/dot_general | solution.py:143
  85.4 16.5 %all-to-all-done.1 = bf16[32,16,1024]{2,0,1:T(8,128)(2,1)S(1)} async-done(((bf16[32,16,1024]{2,0,1:T(8,128)(2,1)}), bf16[32,16,1024]{2,0,1:T(8,128)(2,1)S(1)}, u32[]{:S(2)}, u32[]{:S(2)}) %all-to-all-start.1) | async-done | bytes 1048608 | tf_op jit(solution)/shard_map/all_to_all | solution.py:131
  101.9 5.2 %convolution_convert_fusion = bf16[512,1024]{1,0:T(8,128)(2,1)} fusion(bf16[1024,1024]{1,0:T(8,128)(2,1)} %constant.27, f32[512,1024]{1,0:T(8,128)} %fusion.1, bf16[512,512]{1,0:T(8,128)(2,1)} %bitcast.40, bf16[512,1024]{1,0:T(8,128)(2,1)S(1)} %bitcast.38), kind=kOutput, calls=%fused_computation.3 | convolution fusion | flops 1612709888 | bytes 6815744 | tf_op jit(solution)/shard_map/dot_general | solution.py:59
  107.1 0.0 copy-start
  107.1 0.0 copy-start.2
  107.1 31.8 %all_to_all.35 = bf16[16,32,1024]{2,1,0:T(8,128)(2,1)} all-to-all(bf16[16,32,1024]{2,1,0:T(8,128)(2,1)} %bitcast.39), channel_id=1, replica_groups=mesh['row'=16,'col'=2] {'row'}, dimensions={0} | all-to-all | bytes 2097152 | tf_op jit(solution)/shard_map/all_to_all | solution.py:148
  138.9 0.0 all-gather.6.cloned.1.call-update
  139.0 1.1 dynamic-slice_bitcast_fusion.line_ref
  140.0 32.5 %all-gather.6.cloned.1.call-done.x_ref = bf16[32,32,1024]{2,1,0:T(8,128)(2,1)} async-done(((bf16[16,32,1024]{2,1,0:T(8,128)(2,1)}), bf16[32,32,1024]{2,1,0:T(8,128)(2,1)}) %all-gather.6.cloned.1.call-update) | async-done | bytes 2097168 | tf_op jit(solution)/shard_map/all_gather | solution.py:149
  172.6 0.0 copy-done
  172.6 0.0 copy-done.2
  172.6 0.0 copy-start.1
  172.6 1.6 copy-done.1
  174.2 9.7 %shard_map.104 = (f32[512,1024]{1,0:T(8,128)}, f32[512,1024]{1,0:T(8,128)}) custom-call(bf16[32,32,1024]{2,1,0:T(8,128)(2,1)S(1)} %copy-done.1, bf16[512,512]{1,0:T(8,128)(2,1)S(1)} %copy-done.2, bf16[512,512]{1,0:T(8,128)(2,1)S(1)} %dynamic-slice_bitcast_fusion.line_ref, bf16[1024,1024]{1,0:T(8,128)(2,1)S(1)} %copy-done, bf16[1024,1024]{1,0:T(8,128)(2,1)} %constant.31.sin_ref), custom_call_target="tpu_custom_call" | custom-call | tf_op jit(solution)/shard_map/pallas_call | solution.py:97
  (1 shorter events, 0.0 us)
Async XLA Ops:
  10.3 8.4 %slice-start = ((bf16[32,16384]{1,0:T(8,128)(2,1)}), bf16[32,512]{1,0:T(8,128)(2,1)S(1)}, s32[]{:S(2)}) async-start(bf16[32,16384]{1,0:T(8,128)(2,1)} %param.10), calls=%async_computation.5 | async-start | bytes 65536 | tf_op jit(solution)/shard_map/slice | solution.py:125
  10.3 14.9 %copy-start.3 = (bf16[32,16384]{1,0:T(8,128)(2,1)S(1)}, bf16[32,16384]{1,0:T(8,128)(2,1)}, u32[]{:S(2)}) copy-start(bf16[32,16384]{1,0:T(8,128)(2,1)} %param.10) | copy-start | bytes 3145732
  10.3 51.7 %all-to-all-start = ((bf16[64,16,1024]{2,0,1:T(8,128)(2,1)}), bf16[64,16,1024]{2,0,1:T(8,128)(2,1)S(1)}, u32[]{:S(2)}, u32[]{:S(2)}) async-start(bf16[64,16,1024]{2,0,1:T(8,128)(2,1)} %bitcast.32), calls=%async_computation | async-start | bytes 4194304 | tf_op jit(solution)/shard_map/all_to_all | solution.py:131
  17.8 61.4 %all-gather.8.cloned.1.call-start = ((), (), s32[]{:S(2)}) async-start(), calls=%async_computation.4 | async-start | bytes 1671168 | tf_op jit(solution)/shard_map/all_gather | solution.py:127
  25.2 53.9 %copy-start.4 = (f32[1024]{0:T(1024)S(1)}, f32[1024]{0:T(1024)}, u32[]{:S(2)}) copy-start(f32[1024]{0:T(1024)} %param.11) | copy-start | bytes 12292
  25.2 53.9 %copy-start.5 = (f32[512]{0:T(512)S(1)}, f32[512]{0:T(512)}, u32[]{:S(2)}) copy-start(f32[512]{0:T(512)} %param.12) | copy-start | bytes 6148
  62.0 39.9 %all-to-all-start.1 = ((bf16[32,16,1024]{2,0,1:T(8,128)(2,1)}), bf16[32,16,1024]{2,0,1:T(8,128)(2,1)S(1)}, u32[]{:S(2)}, u32[]{:S(2)}) async-start(bf16[32,16,1024]{2,0,1:T(8,128)(2,1)} %bitcast.30), calls=%async_computation.1 | async-start | bytes 2097152 | tf_op jit(solution)/shard_map/all_to_all | solution.py:131
  79.0 93.5 %all-gather.6.cloned.1.call-start = ((), (), s32[]{:S(2)}) async-start(), calls=%async_computation.3 | async-start | bytes 3145728 | tf_op jit(solution)/shard_map/all_gather | solution.py:149
  107.1 65.5 %copy-start = (bf16[1024,1024]{1,0:T(8,128)(2,1)S(1)}, bf16[1024,1024]{1,0:T(8,128)(2,1)}, u32[]{:S(2)}) copy-start(bf16[1024,1024]{1,0:T(8,128)(2,1)} %constant.30.cos_ref) | copy-start | bytes 6291460
  107.1 65.5 %copy-start.2 = (bf16[512,512]{1,0:T(8,128)(2,1)S(1)}, bf16[512,512]{1,0:T(8,128)(2,1)}, u32[]{:S(2)}) copy-start(bf16[512,512]{1,0:T(8,128)(2,1)} %constant.28.swap_ref) | copy-start | bytes 1572868
  172.6 1.6 copy-start.1
Sparse Core Ops, SparseCore 0:
  25.3 52.7 all-gather.7
  139.1 33.4 all-gather.5

commit v2 on v1

--- a/solution.py
+++ b/solution.py
@@ -111,42 +111,259 @@
     )(x, swap, line_table, cosine, sine)
 
 
+MESH = pl.DeviceIdType.MESH
+
+
+def far_first(count):
+    return sorted(range(1, count), key=lambda k: abs(k - count // 2))
+
+
+def enter(row_count, col_count, row, col):
+    barrier = pltpu.get_barrier_semaphore()
+    for k in range(1, row_count):
+        target = (lax.rem(row + k, row_count), col)
+        pl.semaphore_signal(barrier, inc=1, device_id=target, device_id_type=MESH)
+    for k in range(1, col_count):
+        target = (row, lax.rem(col + k, col_count))
+        pl.semaphore_signal(barrier, inc=1, device_id=target, device_id_type=MESH)
+    pl.semaphore_wait(barrier, row_count + col_count - 2)
+
+
+def send(src, dst, send_sem, recv_sem, target):
+    return pltpu.make_async_remote_copy(
+        src_ref=src,
+        dst_ref=dst,
+        send_sem=send_sem,
+        recv_sem=recv_sem,
+        device_id=target,
+        device_id_type=MESH,
+    )
+
+
+def gather_kernel(
+    row_count,
+    col_count,
+    inner,
+    occ_ref,
+    vir_ref,
+    occ_slab,
+    vir_slab,
+    occ_out,
+    vir_out,
+    occ_rows,
+    vir_rows,
+    wave_send,
+    wave_recv,
+    col_send,
+    col_recv,
+    line_send,
+    line_recv,
+    group_send,
+    group_recv,
+    local,
+):
+    row, col = lax.axis_index("row"), lax.axis_index("col")
+    outer = row_count // inner
+    mine, seat = lax.div(row, inner), lax.rem(row, inner)
+    points = occ_ref.shape[1] // row_count
+    waves = ((occ_ref, occ_out), (vir_ref, vir_out))
+    slabs = ((occ_slab, occ_rows), (vir_slab, vir_rows))
+    enter(row_count, col_count, row, col)
+
+    def block(index):
+        return pl.ds(pl.multiple_of(index * points, LANES), points)
+
+    own = [
+        pltpu.make_async_copy(src.at[:, block(row)], dst.at[row], local.at[i])
+        for i, (src, dst) in enumerate(waves)
+    ]
+    for copy in own:
+        copy.start()
+
+    def over_col(i, k):
+        src, dst = slabs[i]
+        place = dst.at[mine, seat]
+        return send(src, place, col_send.at[i, k], col_recv.at[i, 0], (row, k))
+
+    @pl.when(col == 0)
+    def _():
+        for i, (src, dst) in enumerate(slabs):
+            for k in range(1, col_count):
+                over_col(i, k).start()
+            pltpu.make_async_copy(src, dst.at[mine, seat], local.at[2 + i]).start()
+
+    def wave(i, k):
+        src, dst = waves[i]
+        to = lax.rem(row + k, row_count)
+        return send(
+            src.at[:, block(to)], dst.at[row], wave_send.at[i, k], wave_recv.at[i, k], (to, col)
+        )
+
+    order = far_first(row_count)
+    half = len(order) // 2
+    pending = []
+
+    def start_waves(chosen):
+        for k in chosen:
+            for i in range(2):
+                copy = wave(i, k)
+                copy.start()
+                pending.append(copy)
+
+    start_waves(order[:1])
+
+    @pl.when(col == 0)
+    def _():
+        for i, (src, dst) in enumerate(slabs):
+            pltpu.make_async_copy(src, dst.at[mine, seat], local.at[2 + i]).wait()
+
+    @pl.when(col != 0)
+    def _():
+        for i in range(2):
+            over_col(i, 1).wait_recv()
+
+    lines = []
+    for k in range(1, outer):
+        to = (lax.rem(mine + k, outer) * inner + seat, col)
+        for i in range(2):
+            place = slabs[i][1].at[mine, seat]
+            copy = send(place, place, line_send.at[i, k], line_recv.at[i, k], to)
+            copy.start()
+            lines.append(copy)
+    start_waves(order[1:half])
+    for copy in lines:
+        copy.wait_recv()
+    groups = []
+    for k in range(1, inner):
+        to = (mine * inner + lax.rem(seat + k, inner), col)
+        for i in range(2):
+            place = slabs[i][1].at[:, seat]
+            copy = send(place, place, group_send.at[i, k], group_recv.at[i, k], to)
+            copy.start()
+            groups.append(copy)
+    start_waves(order[half:])
+    for copy in own:
+        copy.wait()
+    for copy in groups:
+        copy.wait()
+    for copy in lines:
+        copy.wait_send()
+
+    @pl.when(col == 0)
+    def _():
+        for i in range(2):
+            for k in range(1, col_count):
+                over_col(i, k).wait_send()
+
+    for copy in pending:
+        copy.wait()
+
+
+def gather(row_count, col_count, occ, vir, occ_slab, vir_slab):
+    inner = 4 if row_count % 4 == 0 else 1
+    points = occ.shape[1] // row_count
+    window = occ_slab.shape[1]
+    outer = row_count // inner
+    shapes = [(row_count, w.shape[0], points) for w in (occ, vir)]
+    shapes += [(outer, inner, w.shape[0], window) for w in (occ, vir)]
+    dma = pltpu.SemaphoreType.DMA
+    return pl.pallas_call(
+        functools.partial(gather_kernel, row_count, col_count, inner),
+        out_shape=[jax.ShapeDtypeStruct(shape, jnp.bfloat16) for shape in shapes],
+        in_specs=[pl.BlockSpec(memory_space=pl.ANY)] * 2
+        + [pl.BlockSpec(memory_space=pltpu.VMEM)] * 2,
+        out_specs=[pl.BlockSpec(memory_space=pltpu.VMEM)] * 4,
+        scratch_shapes=[dma((2, row_count))] * 2
+        + [dma((2, col_count))] * 2
+        + [dma((2, outer))] * 2
+        + [dma((2, inner))] * 2
+        + [dma((4,))],
+        compiler_params=pltpu.CompilerParams(
+            collective_id=0, has_side_effects=True, vmem_limit_bytes=32 * 1024 * 1024
+        ),
+    )(occ, vir, occ_slab, vir_slab)
+
+
+def deliver_kernel(
+    row_count, col_count, p_ref, x_ref, row_send, row_recv, col_send, col_recv, local
+):
+    row, col = lax.axis_index("row"), lax.axis_index("col")
+    enter(row_count, col_count, row, col)
+    order = far_first(row_count)
+    here = x_ref.at[col, row]
+    own = pltpu.make_async_copy(p_ref.at[row], here, local.at[0])
+    own.start()
+    rows = []
+    for k in order:
+        to = lax.rem(row + k, row_count)
+        copy = send(p_ref.at[to], here, row_send.at[k], row_recv.at[k], (to, col))
+        copy.start()
+        rows.append(copy)
+    forwards = []
+
+    def forward(k, src, slot):
+        for d in range(1, col_count):
+            to = (row, lax.rem(col + d, col_count))
+            copy = send(src, slot, col_send.at[d, k], col_recv.at[d, k], to)
+            copy.start()
+            forwards.append(copy)
+
+    forward(0, p_ref.at[row], here)
+    for k, copy in zip(order, rows):
+        copy.wait_recv()
+        slot = x_ref.at[col, lax.rem(row + row_count - k, row_count)]
+        forward(k, slot, slot)
+    own.wait()
+    for copy in rows:
+        copy.wait_send()
+    for copy in forwards:
+        copy.wait()
+
+
+def deliver(row_count, col_count, polar):
+    dma = pltpu.SemaphoreType.DMA
+    return pl.pallas_call(
+        functools.partial(deliver_kernel, row_count, col_count),
+        out_shape=jax.ShapeDtypeStruct((col_count,) + polar.shape, jnp.bfloat16),
+        in_specs=[pl.BlockSpec(memory_space=pltpu.VMEM)],
+        out_specs=pl.BlockSpec(memory_space=pltpu.VMEM),
+        scratch_shapes=[dma((row_count,))] * 2 + [dma((col_count, row_count))] * 2 + [dma((1,))],
+        compiler_params=pltpu.CompilerParams(
+            collective_id=1, has_side_effects=True, vmem_limit_bytes=32 * 1024 * 1024
+        ),
+    )(polar)
+
+
 def on_device(rows_dev, occupied_waves, virtual_waves, occupied_decay, virtual_decay):
     row_count = lax.axis_size("row")
     col_count = lax.axis_size("col")
-    occ_share = occupied_waves.shape[0]
-    share = occ_share + virtual_waves.shape[0]
     nocc, nvir = occupied_decay.shape[0], virtual_decay.shape[0]
     window = rows_dev * row_count
     points = occupied_waves.shape[1] // row_count
     contract = (((0,), (0,)), ((), ()))
     factor = -1.0 / math.sqrt(nocc * nvir) / math.sqrt(NGRID)
 
-    first = jnp.concatenate([occupied_waves[:, :window], virtual_waves[:, :window]], axis=0)
-    first = lax.all_gather(first, "col")[0]
-    first = lax.all_gather(first, "row")
-
-    def exchange(waves):
-        shaped = waves.reshape(waves.shape[0], row_count, points)
-        shaped = lax.all_to_all(shaped, "row", split_axis=1, concat_axis=0, tiled=True)
-        return shaped.reshape(waves.shape[0] * row_count, points)
-
-    plane_occ = exchange(occupied_waves)
-    plane_vir = exchange(virtual_waves)
-
-    def scaled(rows, decay):
-        rows = rows.reshape(decay.shape[0], window).astype(jnp.float32)
-        return (rows * decay[:, None]).astype(jnp.bfloat16)
-
-    occ_rows = scaled(first[:, :occ_share], occupied_decay)
-    vir_rows = scaled(first[:, occ_share:], virtual_decay)
+    def slab(waves, decay):
+        share = waves.shape[0]
+        own = lax.dynamic_slice_in_dim(decay, lax.axis_index("row") * share, share)
+        return (waves[:, :window].astype(jnp.float32) * own[:, None]).astype(jnp.bfloat16)
+
+    plane_occ, plane_vir, occ_rows, vir_rows = gather(
+        row_count,
+        col_count,
+        occupied_waves,
+        virtual_waves,
+        slab(occupied_waves, occupied_decay),
+        slab(virtual_waves, virtual_decay),
+    )
+    plane_occ, plane_vir = plane_occ.reshape(nocc, points), plane_vir.reshape(nvir, points)
+    occ_rows, vir_rows = occ_rows.reshape(nocc, window), vir_rows.reshape(nvir, window)
     green_occ = lax.dot_general(occ_rows, plane_occ, contract, preferred_element_type=jnp.float32)
     green_vir = lax.dot_general(vir_rows, plane_vir, contract, preferred_element_type=jnp.float32)
     polar = (green_occ * green_vir * factor).astype(jnp.bfloat16)
     polar = dot(polar, swap_table(points // NC, NC, 1)).astype(jnp.bfloat16)
     polar = polar.reshape(row_count, rows_dev, points)
-    polar = lax.all_to_all(polar, "row", split_axis=0, concat_axis=0, tiled=True)
-    polar = lax.all_gather(polar, "col")
+    polar = deliver(row_count, col_count, polar)
     pieces = points == NB * NC
     if pieces:
         x = polar.reshape(col_count * row_count, rows_dev, points)

time: 191 us -> 162 us (0.85)
  Pallas kernels: 9.66 us -> 145 us
  waiting for transfers between devices: 84.7 us -> 0 us
  blocking collectives: 37.6 us -> 0 us
  starting transfers between devices: 24.6 us -> 0 us
  between operations: 14.1 us -> 0.69 us
    pallas_call x0 -> x2, Pallas kernels: none -> 135 us  [the longest x1 93.4 us: gather(): pl.pallas_call(functools.partial(gather_kernel, row_count, col_count, inn...]
    all_to_all x2 -> x0, waiting for transfers between devices: 52.2 us -> none  [exchange(): lax.all_to_all(shaped, 'row', split_axis=1, concat_axis=0, tiled=True)]
    all_gather x2 -> x0, waiting for transfers between devices: 32.5 us -> none  [the longest x1 32.5 us: on_device(): polar = lax.all_gather(polar, 'col')]
    all_to_all x1 -> x0, blocking collectives: 31.8 us -> none  [on_device(): lax.all_to_all(polar, 'row', split_axis=0, concat_axis=0, tiled=True)]
    all_to_all x2 -> x0, starting transfers between devices: 24.6 us -> none  [exchange(): lax.all_to_all(shaped, 'row', split_axis=1, concat_axis=0, tiled=True)]
    all_gather x1 -> x0, blocking collectives: 5.77 us -> none  [on_device(): first = lax.all_gather(first, 'col')[0]]
    reshape x2 -> x0, local copies, waits for them, and re-layouts: 4.22 us -> none  [exchange(): shaped = waves.reshape(waves.shape[0], row_count, points)]
    unnamed x12 -> x8, local copies, waits for them, and re-layouts: 1.62 us -> 5.44 us
  transfers between devices with their start and end apart: 4 -> 0, of which waited for: 3 -> 0; matrix products, arithmetic and copies ran while one was open for 5% -> 0% of each run, Pallas kernels for 0% -> 0%
where the time goes in v2:
time: 162 us
  Pallas kernels  145 us (90%)
  local copies, waits for them, and re-layouts  8.05 us (5%)
  matrix products  6.62 us (4%)
  other arithmetic  1.75 us (1%)
    pallas_call x1, Pallas kernels, gather(): pl.pallas_call(functools.partial(gather_kernel, row_count, col_count, inn...  93.4 us
    pallas_call x1, Pallas kernels, deliver(): pl.pallas_call(functools.partial(deliver_kernel, row_count, col_count), o...  41.7 us
    pallas_call x1, Pallas kernels, spectrum(): pl.pallas_call(functools.partial(spectrum_kernel, pieces), grid=(steps,),...  9.67 us
    unnamed x8, local copies, waits for them, and re-layouts  5.44 us
    dot_general x1, matrix products, dot(): return jnp.dot(a, b, preferred_element_type=jnp.float32)  4.04 us

profile of v2, /device:TPU:0, one launch (start us, length us, event | category | flops | bytes accessed | tf_op | source)
XLA Modules:
  0.0 161.8 jit_solution(194315099189083655)
XLA Ops:
  0.6 0.8 dynamic_slice.10
  1.4 0.9 multiply_convert_fusion.1.occ_slab
  2.3 0.8 dynamic_slice.11
  3.1 0.8 multiply_convert_fusion.2.vir_slab
  3.9 0.0 copy-start
  3.9 1.6 copy-done
  5.5 0.0 copy-start.2
  5.5 1.2 copy-done.2
  6.7 93.4 %shard_map.104 = (bf16[16,64,1024]{2,1,0:T(8,128)(2,1)S(1)}, bf16[16,32,1024]{2,1,0:T(8,128)(2,1)S(1)}, bf16[4,4,64,512]{3,2,1,0:T(8,128)(2,1)S(1)}, bf16[4,4,32,512]{3,2,1,0:T(8,128)(2,1)S(1)}) custom-call(bf16[64,16384]{1,0:T(8,128)(2,1)S(1)} %copy-done, bf16[32,16384]{1,0:T(8,128)(2,1)S(1)} %copy-done.2, ...), custom_call_target="tpu_custom_call" | custom-call | tf_op jit(solution)/shard_map/pallas_call | solution.py:270
  100.1 2.6 %fusion.1 = f32[512,1024]{1,0:T(8,128)} fusion(bf16[1024,512]{1,0:T(8,128)(2,1)S(1)} %bitcast.17, bf16[1024,1024]{1,0:T(8,128)(2,1)S(1)} %bitcast.16), kind=kOutput, calls=%fused_computation.6 | convolution fusion | flops 1073741824 | bytes 5242880 | tf_op jit(solution)/shard_map/dot_general | solution.py:361
  102.7 4.0 %convolution_convert_fusion = bf16[512,1024]{1,0:T(8,128)(2,1)S(1)} fusion(bf16[1024,1024]{1,0:T(8,128)(2,1)} %constant.40, f32[512,1024]{1,0:T(8,128)} %fusion.1, bf16[512,512]{1,0:T(8,128)(2,1)S(1)} %bitcast.20, bf16[512,1024]{1,0:T(8,128)(2,1)S(1)} %bitcast.19), kind=kOutput, calls=%fused_computation.1 | convolution fusion | flops 1612709888 | bytes 6815744 | tf_op jit(solution)/shard_map/dot_general | solution.py:59
  106.7 41.7 %shard_map.105 = bf16[2,16,32,1024]{3,2,1,0:T(8,128)(2,1)S(1)} custom-call(bf16[16,32,1024]{2,1,0:T(8,128)(2,1)S(1)} %bitcast.18), custom_call_target="tpu_custom_call" | custom-call | tf_op jit(solution)/shard_map/pallas_call | solution.py:325
  148.4 1.1 dynamic-slice_bitcast_fusion.line_ref
  149.5 0.0 copy-start.1
  149.5 1.6 copy-done.1
  151.1 0.0 copy-start.3
  151.1 1.0 copy-done.3
  152.1 9.7 %shard_map.106 = (f32[512,1024]{1,0:T(8,128)}, f32[512,1024]{1,0:T(8,128)}) custom-call(bf16[32,32,1024]{2,1,0:T(8,128)(2,1)S(1)} %bitcast.15, bf16[512,512]{1,0:T(8,128)(2,1)S(1)} %copy-done.3, bf16[512,512]{1,0:T(8,128)(2,1)S(1)} %dynamic-slice_bitcast_fusion.line_ref, bf16[1024,1024]{1,0:T(8,128)(2,1)S(1)} %copy-done.1, bf16[1024,1024]{1,0:T(8,128)(2,1)} %constant.44.sin_ref), custom_call_target="tpu_custom_call" | custom-call | tf_op jit(solution)/shard_map/pallas_call | solution.py:97
Async XLA Ops:
  3.9 1.6 copy-start
  5.5 1.2 copy-start.2
  149.5 1.6 copy-start.1
  151.1 1.0 copy-start.3

commit v3 on v2

--- a/solution.py
+++ b/solution.py
@@ -114,8 +114,15 @@
 MESH = pl.DeviceIdType.MESH
 
 
-def far_first(count):
-    return sorted(range(1, count), key=lambda k: abs(k - count // 2))
+def flip(index, mask):
+    bits = [1 << bit for bit in range(mask.bit_length()) if mask >> bit & 1]
+    for bit in bits:
+        index = index + bit - 2 * bit * lax.rem(lax.div(index, bit), 2)
+    return index
+
+
+def group_size(row_count):
+    return 4 if row_count % 4 == 0 else 1
 
 
 def enter(row_count, col_count, row, col):
@@ -192,25 +199,27 @@
                 over_col(i, k).start()
             pltpu.make_async_copy(src, dst.at[mine, seat], local.at[2 + i]).start()
 
-    def wave(i, k):
-        src, dst = waves[i]
-        to = lax.rem(row + k, row_count)
-        return send(
-            src.at[:, block(to)], dst.at[row], wave_send.at[i, k], wave_recv.at[i, k], (to, col)
-        )
-
-    order = far_first(row_count)
-    half = len(order) // 2
     pending = []
 
-    def start_waves(chosen):
-        for k in chosen:
-            for i in range(2):
-                copy = wave(i, k)
+    def start_waves(far, steps=range(inner)):
+        for step in steps:
+            if far == 0 and step == 0:
+                continue
+            k = far * inner + step
+            there = flip(mine, far)
+            to = there * inner + lax.rem(seat + step, inner)
+            for i, (src, dst) in enumerate(waves):
+                copy = send(
+                    src.at[:, block(to)],
+                    dst.at[row],
+                    wave_send.at[i, k],
+                    wave_recv.at[i, k],
+                    (to, col),
+                )
                 copy.start()
                 pending.append(copy)
 
-    start_waves(order[:1])
+    start_waves(0)
 
     @pl.when(col == 0)
     def _():
@@ -223,16 +232,34 @@
             over_col(i, 1).wait_recv()
 
     lines = []
-    for k in range(1, outer):
-        to = (lax.rem(mine + k, outer) * inner + seat, col)
-        for i in range(2):
-            place = slabs[i][1].at[mine, seat]
-            copy = send(place, place, line_send.at[i, k], line_recv.at[i, k], to)
+    bits = [1 << bit for bit in reversed(range((outer - 1).bit_length()))]
+    early = inner // 2
+
+    def double(held, bit):
+        to = (flip(mine, bit) * inner + seat, col)
+        started = []
+        for mask in held:
+            for i in range(2):
+                place = slabs[i][1].at[flip(mine, mask), seat]
+                k = bit + mask
+                started.append(send(place, place, line_send.at[i, k], line_recv.at[i, k], to))
+        for copy in started:
             copy.start()
-            lines.append(copy)
-    start_waves(order[1:half])
-    for copy in lines:
-        copy.wait_recv()
+        lines.extend(started)
+        return started
+
+    held = [0]
+    for number, bit in enumerate(bits):
+        started = double(held, bit)
+        if number == 0:
+            start_waves(bits[0], range(early))
+        held = held + [mask + bit for mask in held]
+        if number == len(bits) - 1:
+            for far in range(1, bits[0]):
+                start_waves(far)
+            start_waves(bits[0], range(early, inner))
+        for copy in started:
+            copy.wait_recv()
     groups = []
     for k in range(1, inner):
         to = (mine * inner + lax.rem(seat + k, inner), col)
@@ -241,7 +268,8 @@
             copy = send(place, place, group_send.at[i, k], group_recv.at[i, k], to)
             copy.start()
             groups.append(copy)
-    start_waves(order[half:])
+    for far in range(bits[0] + 1 if bits else 1, outer):
+        start_waves(far)
     for copy in own:
         copy.wait()
     for copy in groups:
@@ -260,7 +288,7 @@
 
 
 def gather(row_count, col_count, occ, vir, occ_slab, vir_slab):
-    inner = 4 if row_count % 4 == 0 else 1
+    inner = group_size(row_count)
     points = occ.shape[1] // row_count
     window = occ_slab.shape[1]
     outer = row_count // inner
@@ -289,13 +317,15 @@
 ):
     row, col = lax.axis_index("row"), lax.axis_index("col")
     enter(row_count, col_count, row, col)
-    order = far_first(row_count)
+    inner = group_size(row_count)
+    mine, seat = lax.div(row, inner), lax.rem(row, inner)
     here = x_ref.at[col, row]
     own = pltpu.make_async_copy(p_ref.at[row], here, local.at[0])
     own.start()
     rows = []
+    order = range(1, row_count)
     for k in order:
-        to = lax.rem(row + k, row_count)
+        to = flip(mine, k // inner) * inner + lax.rem(seat + k % inner, inner)
         copy = send(p_ref.at[to], here, row_send.at[k], row_recv.at[k], (to, col))
         copy.start()
         rows.append(copy)
@@ -311,7 +341,8 @@
     forward(0, p_ref.at[row], here)
     for k, copy in zip(order, rows):
         copy.wait_recv()
-        slot = x_ref.at[col, lax.rem(row + row_count - k, row_count)]
+        source = flip(mine, k // inner) * inner + lax.rem(seat + inner - k % inner, inner)
+        slot = x_ref.at[col, source]
         forward(k, slot, slot)
     own.wait()
     for copy in rows:

time: 162 us -> 142 us (0.88)
  Pallas kernels: 145 us -> 125 us
    pallas_call x1, Pallas kernels: 93.4 us -> 68.8 us  [gather(): pl.pallas_call(functools.partial(gather_kernel, row_count, col_count, inn...]
    pallas_call x1, Pallas kernels: 41.7 us -> 46.2 us  [deliver(): pl.pallas_call(functools.partial(deliver_kernel, row_count, col_count), o...]
where the time goes in v3:
time: 142 us
  Pallas kernels  125 us (88%)
  local copies, waits for them, and re-layouts  8.05 us (6%)
  matrix products  6.62 us (5%)
  other arithmetic  1.75 us (1%)
    pallas_call x1, Pallas kernels, gather(): pl.pallas_call(functools.partial(gather_kernel, row_count, col_count, inn...  68.8 us
    pallas_call x1, Pallas kernels, deliver(): pl.pallas_call(functools.partial(deliver_kernel, row_count, col_count), o...  46.2 us
    pallas_call x1, Pallas kernels, spectrum(): pl.pallas_call(functools.partial(spectrum_kernel, pieces), grid=(steps,),...  9.66 us
    unnamed x8, local copies, waits for them, and re-layouts  5.44 us
    dot_general x1, matrix products, dot(): return jnp.dot(a, b, preferred_element_type=jnp.float32)  4.03 us

profile of v3, /device:TPU:0, one launch (start us, length us, event | category | flops | bytes accessed | tf_op | source)
XLA Modules:
  0.0 141.8 jit_solution(12374190278841993000)
XLA Ops:
  0.6 0.8 dynamic_slice.10
  1.4 0.9 multiply_convert_fusion.1.occ_slab
  2.3 0.8 dynamic_slice.11
  3.1 0.8 multiply_convert_fusion.2.vir_slab
  3.9 0.0 copy-start
  3.9 1.6 %copy-done = bf16[64,16384]{1,0:T(8,128)(2,1)S(1)} copy-done((bf16[64,16384]{1,0:T(8,128)(2,1)S(1)}, bf16[64,16384]{1,0:T(8,128)(2,1)}, u32[]{:S(2)}) %copy-start) | copy-done | bytes 2097176
  5.5 0.0 copy-start.2
  5.5 1.2 copy-done.2
  6.7 68.8 %shard_map.104 = (bf16[16,64,1024]{2,1,0:T(8,128)(2,1)S(1)}, bf16[16,32,1024]{2,1,0:T(8,128)(2,1)S(1)}, bf16[4,4,64,512]{3,2,1,0:T(8,128)(2,1)S(1)}, bf16[4,4,32,512]{3,2,1,0:T(8,128)(2,1)S(1)}) custom-call(bf16[64,16384]{1,0:T(8,128)(2,1)S(1)} %copy-done, bf16[32,16384]{1,0:T(8,128)(2,1)S(1)} %copy-done.2, ...), custom_call_target="tpu_custom_call" | custom-call | tf_op jit(solution)/shard_map/pallas_call | solution.py:298
  75.5 2.6 %fusion.1 = f32[512,1024]{1,0:T(8,128)} fusion(bf16[1024,512]{1,0:T(8,128)(2,1)S(1)} %bitcast.17, bf16[1024,1024]{1,0:T(8,128)(2,1)S(1)} %bitcast.16), kind=kOutput, calls=%fused_computation.6 | convolution fusion | flops 1073741824 | bytes 5242880 | tf_op jit(solution)/shard_map/dot_general | solution.py:392
  78.1 4.0 %convolution_convert_fusion = bf16[512,1024]{1,0:T(8,128)(2,1)S(1)} fusion(bf16[1024,1024]{1,0:T(8,128)(2,1)} %constant.40, f32[512,1024]{1,0:T(8,128)} %fusion.1, bf16[512,512]{1,0:T(8,128)(2,1)S(1)} %bitcast.20, bf16[512,1024]{1,0:T(8,128)(2,1)S(1)} %bitcast.19), kind=kOutput, calls=%fused_computation.1 | convolution fusion | flops 1612709888 | bytes 6815744 | tf_op jit(solution)/shard_map/dot_general | solution.py:59
  82.2 46.2 %shard_map.105 = bf16[2,16,32,1024]{3,2,1,0:T(8,128)(2,1)S(1)} custom-call(bf16[16,32,1024]{2,1,0:T(8,128)(2,1)S(1)} %bitcast.18), custom_call_target="tpu_custom_call" | custom-call | tf_op jit(solution)/shard_map/pallas_call | solution.py:356
  128.4 1.1 dynamic-slice_bitcast_fusion.line_ref
  129.5 0.0 copy-start.1
  129.5 1.6 %copy-done.1 = bf16[1024,1024]{1,0:T(8,128)(2,1)S(1)} copy-done((bf16[1024,1024]{1,0:T(8,128)(2,1)S(1)}, bf16[1024,1024]{1,0:T(8,128)(2,1)}, u32[]{:S(2)}) %copy-start.1) | copy-done | bytes 2097176
  131.1 0.0 copy-start.3
  131.1 1.0 copy-done.3
  132.1 9.7 %shard_map.106 = (f32[512,1024]{1,0:T(8,128)}, f32[512,1024]{1,0:T(8,128)}) custom-call(bf16[32,32,1024]{2,1,0:T(8,128)(2,1)S(1)} %bitcast.15, bf16[512,512]{1,0:T(8,128)(2,1)S(1)} %copy-done.3, bf16[512,512]{1,0:T(8,128)(2,1)S(1)} %dynamic-slice_bitcast_fusion.line_ref, bf16[1024,1024]{1,0:T(8,128)(2,1)S(1)} %copy-done.1, bf16[1024,1024]{1,0:T(8,128)(2,1)} %constant.44.sin_ref), custom_call_target="tpu_custom_call" | custom-call | tf_op jit(solution)/shard_map/pallas_call | solution.py:97
Async XLA Ops:
  3.9 1.6 %copy-start = (bf16[64,16384]{1,0:T(8,128)(2,1)S(1)}, bf16[64,16384]{1,0:T(8,128)(2,1)}, u32[]{:S(2)}) copy-start(bf16[64,16384]{1,0:T(8,128)(2,1)} %occ_ref.1) | copy-start | bytes 6291460
  5.5 1.2 copy-start.2
  129.5 1.6 %copy-start.1 = (bf16[1024,1024]{1,0:T(8,128)(2,1)S(1)}, bf16[1024,1024]{1,0:T(8,128)(2,1)}, u32[]{:S(2)}) copy-start(bf16[1024,1024]{1,0:T(8,128)(2,1)} %constant.43.cos_ref) | copy-start | bytes 6291460
  131.1 1.0 copy-start.3

commit v4 on v3

--- a/solution.py
+++ b/solution.py
@@ -77,7 +77,7 @@
                     ]
     else:
         rows[...] = x_ref[...].reshape(NC * R_BLOCK, NAB)
-    line = dot(line_ref[...], rows[...]).astype(jnp.bfloat16)
+    line = dot(line_ref[lax.axis_index("col")], rows[...]).astype(jnp.bfloat16)
     half = line.shape[0] // 2
     re, im = line[:half], line[half:]
     re_ref[...] = dot(re, cos_ref[...]) + dot(im, sin_ref[...])
@@ -89,9 +89,9 @@
     cosine, sine = plane_tables()
     per = LANES // NB
     swap = swap_table(per, per, NB)
-    out_rows = line_table.shape[0] // 2
+    out_rows = line_table.shape[1] // 2
     steps = r_count // R_BLOCK
-    whole = lambda table: pl.BlockSpec(table.shape, lambda i: (0, 0))
+    whole = lambda table: pl.BlockSpec(table.shape, lambda i: (0,) * table.ndim)
     out = jax.ShapeDtypeStruct((out_rows * steps, NAB), jnp.float32)
     out_spec = pl.BlockSpec((out_rows, NAB), lambda i: (i, 0))
     return pl.pallas_call(
@@ -298,7 +298,7 @@
     return pl.pallas_call(
         functools.partial(gather_kernel, row_count, col_count, inner),
         out_shape=[jax.ShapeDtypeStruct(shape, jnp.bfloat16) for shape in shapes],
-        in_specs=[pl.BlockSpec(memory_space=pl.ANY)] * 2
+        in_specs=[pl.BlockSpec(memory_space=pltpu.HBM)] * 2
         + [pl.BlockSpec(memory_space=pltpu.VMEM)] * 2,
         out_specs=[pl.BlockSpec(memory_space=pltpu.VMEM)] * 4,
         scratch_shapes=[dma((2, row_count))] * 2
@@ -359,6 +359,9 @@
         in_specs=[pl.BlockSpec(memory_space=pltpu.VMEM)],
         out_specs=pl.BlockSpec(memory_space=pltpu.VMEM),
         scratch_shapes=[dma((row_count,))] * 2 + [dma((col_count, row_count))] * 2 + [dma((1,))],
+        cost_estimate=pl.CostEstimate(
+            flops=0, bytes_accessed=32 * polar.size * col_count, transcendentals=0
+        ),
         compiler_params=pltpu.CompilerParams(
             collective_id=1, has_side_effects=True, vmem_limit_bytes=32 * 1024 * 1024
         ),
@@ -401,8 +404,7 @@
     else:
         x = polar.reshape(col_count * row_count, rows_dev, NC, points // NC)
         x = jnp.transpose(x, (2, 1, 0, 3)).reshape(NC, rows_dev, NAB)
-    table = lax.dynamic_index_in_dim(line_tables(col_count), lax.axis_index("col"), 0, False)
-    real_part, imag_part = spectrum(pieces, x, table)
+    real_part, imag_part = spectrum(pieces, x, line_tables(col_count))
     shape = (rows_dev, NC // col_count, NAB)
     return real_part.reshape(shape), imag_part.reshape(shape)
 

time: 142 us -> 139 us (0.979)
  local copies, waits for them, and re-layouts: 8.05 us -> 4.35 us
    unnamed x8 -> x10, local copies, waits for them, and re-layouts: 5.44 us -> 2.83 us
where the time goes in v4:
time: 139 us; the launch traced here: 138 us
  Pallas kernels  125 us (90%)
  matrix products  6.68 us (5%)
  local copies, waits for them, and re-layouts  4.35 us (3%)
  other arithmetic  1.75 us (1%)
    pallas_call x1, Pallas kernels, gather(): pl.pallas_call(functools.partial(gather_kernel, row_count, col_count, inn...  68.8 us
    pallas_call x1, Pallas kernels, deliver(): pl.pallas_call(functools.partial(deliver_kernel, row_count, col_count), o...  46.2 us
    pallas_call x1, Pallas kernels, spectrum(): pl.pallas_call(functools.partial(spectrum_kernel, pieces), grid=(steps,),...  9.68 us
    dot_general x1, matrix products, dot(): return jnp.dot(a, b, preferred_element_type=jnp.float32)  4.09 us
    unnamed x10, local copies, waits for them, and re-layouts  2.83 us

profile of v4, /device:TPU:0, one launch (start us, length us, event | category | flops | bytes accessed | tf_op | source)
XLA Modules:
  0.0 138.2 jit_solution(5737233243685717459)
XLA Ops:
  0.6 0.8 dynamic_slice.7
  1.4 0.8 dynamic_slice.6
  2.2 0.8 multiply_convert_fusion.2.vir_slab
  3.0 0.9 multiply_convert_fusion.1.occ_slab
  3.9 0.0 copy-start
  3.9 1.6 %copy-done = bf16[64,16384]{1,0:T(8,128)(2,1)S(1)} copy-done((bf16[64,16384]{1,0:T(8,128)(2,1)S(1)}, bf16[64,16384]{1,0:T(8,128)(2,1)}, u32[]{:S(2)}) %copy-start) | copy-done | bytes 2097176
  5.5 0.0 copy-start.2
  5.5 1.2 copy-done.2
  6.7 68.8 %shard_map.104 = (bf16[16,64,1024]{2,1,0:T(8,128)(2,1)S(1)}, bf16[16,32,1024]{2,1,0:T(8,128)(2,1)S(1)}, bf16[4,4,64,512]{3,2,1,0:T(8,128)(2,1)S(1)}, bf16[4,4,32,512]{3,2,1,0:T(8,128)(2,1)S(1)}) custom-call(bf16[64,16384]{1,0:T(8,128)(2,1)S(1)} %copy-done, bf16[32,16384]{1,0:T(8,128)(2,1)S(1)} %copy-done.2, ...), custom_call_target="tpu_custom_call" | custom-call | tf_op jit(solution)/shard_map/pallas_call | solution.py:298
  75.5 2.6 %fusion.1 = f32[512,1024]{1,0:T(8,128)} fusion(bf16[1024,512]{1,0:T(8,128)(2,1)S(1)} %bitcast.15, bf16[1024,1024]{1,0:T(8,128)(2,1)S(1)} %bitcast.14), kind=kOutput, calls=%fused_computation.5 | convolution fusion | flops 1073741824 | bytes 5242880 | tf_op jit(solution)/shard_map/dot_general | solution.py:395
  78.1 0.0 copy-start.4
  78.1 4.1 %convolution_convert_fusion = bf16[512,1024]{1,0:T(8,128)(2,1)S(1)} fusion(bf16[1024,1024]{1,0:T(8,128)(2,1)} %constant.33, f32[512,1024]{1,0:T(8,128)} %fusion.1, bf16[512,512]{1,0:T(8,128)(2,1)S(1)} %bitcast.18, bf16[512,1024]{1,0:T(8,128)(2,1)S(1)} %bitcast.17), kind=kOutput, calls=%fused_computation.1 | convolution fusion | flops 1612709888 | bytes 6815744 | tf_op jit(solution)/shard_map/dot_general | solution.py:59
  82.2 0.0 copy-start.1
  82.2 0.0 copy-start.3
  82.3 46.2 %shard_map.105 = bf16[2,16,32,1024]{3,2,1,0:T(8,128)(2,1)S(1)} custom-call(bf16[16,32,1024]{2,1,0:T(8,128)(2,1)S(1)} %bitcast.16), custom_call_target="tpu_custom_call" | custom-call | bytes 33554432 | tf_op jit(solution)/shard_map/pallas_call | solution.py:356
  128.5 0.0 copy-done.4
  128.5 0.0 copy-done.1
  128.5 0.0 copy-done.3
  128.5 9.7 %shard_map.106 = (f32[512,1024]{1,0:T(8,128)}, f32[512,1024]{1,0:T(8,128)}) custom-call(bf16[32,32,1024]{2,1,0:T(8,128)(2,1)S(1)} %bitcast.13, bf16[512,512]{1,0:T(8,128)(2,1)S(1)} %copy-done.4, bf16[2,512,512]{2,1,0:T(8,128)(2,1)S(1)} %copy-done.3, bf16[1024,1024]{1,0:T(8,128)(2,1)S(1)} %copy-done.1, bf16[1024,1024]{1,0:T(8,128)(2,1)} %constant.37.sin_ref), custom_call_target="tpu_custom_call" | custom-call | tf_op jit(solution)/shard_map/pallas_call | solution.py:97
Async XLA Ops:
  3.9 1.6 %copy-start = (bf16[64,16384]{1,0:T(8,128)(2,1)S(1)}, bf16[64,16384]{1,0:T(8,128)(2,1)}, u32[]{:S(2)}) copy-start(bf16[64,16384]{1,0:T(8,128)(2,1)} %occ_ref.1) | copy-start | bytes 6291460
  5.5 1.2 copy-start.2
  78.1 50.4 %copy-start.4 = (bf16[512,512]{1,0:T(8,128)(2,1)S(1)}, bf16[512,512]{1,0:T(8,128)(2,1)}, u32[]{:S(2)}) copy-start(bf16[512,512]{1,0:T(8,128)(2,1)} %constant.34.swap_ref) | copy-start | bytes 1572868
  82.2 46.3 %copy-start.1 = (bf16[1024,1024]{1,0:T(8,128)(2,1)S(1)}, bf16[1024,1024]{1,0:T(8,128)(2,1)}, u32[]{:S(2)}) copy-start(bf16[1024,1024]{1,0:T(8,128)(2,1)} %constant.36.cos_ref) | copy-start | bytes 6291460
  82.2 46.3 %copy-start.3 = (bf16[2,512,512]{2,1,0:T(8,128)(2,1)S(1)}, bf16[2,512,512]{2,1,0:T(8,128)(2,1)}, u32[]{:S(2)}) copy-start(bf16[2,512,512]{2,1,0:T(8,128)(2,1)} %constant.35.line_ref) | copy-start | bytes 3145732
